TPU v7x, 8 devices: a whole 2x2x1 slice. The times are simulated.
8 devices in a mesh: dp: 1 (over z), ep: 8 (over y, x, core).
Axes of the slice: x: 2, y: 2, z: 1, core: 2. Of those that a mesh axis runs over, the one named last changes fastest.
Arguments:
- x_rows: bfloat16 [8192, 768], P(('dp', 'ep'))
- sel_idx: int32 [64, 256], P(('dp', 'ep'))
- gate_w: float32 [64, 256], P(('dp', 'ep'))
- w_up: bfloat16 [64, 768, 3072], P('ep')
- w_down: bfloat16 [64, 3072, 768], P('ep')
Outputs:
- output: bfloat16 [8192, 768], P(('dp', 'ep'))
All inputs are finite; a program needn't handle non-finite values.
Results may differ from a plain program's by a relative error of at most 0.00676407.
Values are sent between devices in bfloat16 or wider.
A program may use at most 1 GiB of HBM per device.

v0:
```python
import jax
import jax.numpy as jnp
from jax import lax
from jax.sharding import PartitionSpec as P


def solution(mesh):
    group_size = mesh.shape["ep"]

    def local_layer(x_loc, sel_loc, gate_loc, up_loc, down_loc):
        tok_loc, model_width = x_loc.shape
        exp_loc, cap_rows = sel_loc.shape
        entry_count = exp_loc * cap_rows
        pair_cap = 2 * entry_count // group_size
        flat_sel = sel_loc.reshape(entry_count)
        src_dev = flat_sel // tok_loc
        local_row = flat_sel - src_dev * tok_loc
        sort_order = jnp.argsort(src_dev, stable=True)
        position = jnp.argsort(sort_order)
        counts = jnp.bincount(src_dev, length=group_size)
        starts = jnp.cumsum(counts) - counts
        slot_idx = src_dev * pair_cap + position - starts[src_dev]
        request = jnp.zeros((group_size * pair_cap,), jnp.int32).at[slot_idx].set(local_row, unique_indices=True)
        wanted = lax.all_to_all(request.reshape(group_size, pair_cap), "ep", 0, 0, tiled=True).reshape(group_size * pair_cap)
        send_rows = jnp.take(x_loc, wanted, axis=0).reshape(group_size, pair_cap, model_width)
        received = lax.all_to_all(send_rows, "ep", 0, 0, tiled=True).reshape(group_size * pair_cap, model_width)
        picked = jnp.take(received, slot_idx, axis=0).reshape(exp_loc, cap_rows, model_width)
        hidden = jax.nn.gelu(jnp.einsum("ecd,edf->ecf", picked, up_loc, preferred_element_type=jnp.float32), approximate=True).astype(jnp.bfloat16)
        out_rows = jnp.einsum("ecf,efd->ecd", hidden, down_loc, preferred_element_type=jnp.float32)
        contrib = (out_rows * gate_loc[:, :, None]).astype(jnp.bfloat16).reshape(entry_count, model_width)
        back_rows = jnp.zeros((group_size * pair_cap, model_width), jnp.bfloat16).at[slot_idx].set(contrib, unique_indices=True)
        returned = lax.all_to_all(back_rows.reshape(group_size, pair_cap, model_width), "ep", 0, 0, tiled=True).reshape(group_size * pair_cap, model_width)
        summed = jax.ops.segment_sum(returned.astype(jnp.float32), wanted, num_segments=tok_loc)
        return (x_loc.astype(jnp.float32) + summed).astype(jnp.bfloat16)

    row_spec = P(("dp", "ep"), None)
    weight_spec = P("ep", None, None)
    return jax.shard_map(local_layer, mesh=mesh, in_specs=(row_spec, row_spec, row_spec, weight_spec, weight_spec), out_specs=row_spec, check_vma=False)
```

profile of v0, /device:TPU:0, one launch (start us, length us, event | category | flops | bytes accessed | tf_op | source)
XLA Modules:
  0.0 318.5 jit_solution(8989511965862256699)
XLA Ops:
  0.0 0.7 copy.8
  0.8 14.7 %scatter_custom_fusion = s32[8]{0:T(128)S(1)} fusion(s32[2048]{0:T(1024)S(1)} %bitcast.49, s32[2048]{0:T(1024)S(1)} %ne.44, s32[]{:T(128)} %constant.26.clone.1), kind=kCustom, calls=%fused_computation.62 | custom fusion | flops 2048 | bytes 36 | tf_op jit(solution)/shard_map/scatter-add | solution.py:20
  15.4 0.2 reduce-window.9
  15.6 0.7 fusion.44
  16.3 0.7 copy.7
  17.1 5.0 %sort.34 = (s32[2048]{0:T(1024)}, s32[2048]{0:T(1024)S(1)}) sort(s32[2048]{0:T(1024)S(1)} %get-tuple-element.14, s32[2048]{0:T(1024)S(1)} %iota.8), dimensions={0}, to_apply=%region_0.1 | sort | flops 22528 | bytes 32768 | tf_op jit(solution)/shard_map/jit(argsort)/sort | solution.py:18
  22.1 5.0 %sort.35 = (s32[2048]{0:T(1024)}, s32[2048]{0:T(1024)S(1)}) sort(s32[2048]{0:T(1024)S(1)} %get-tuple-element.7, s32[2048]{0:T(1024)S(1)} %iota.9), dimensions={0}, to_apply=%region_1.2 | sort | flops 22528 | bytes 32768 | tf_op jit(solution)/shard_map/jit(argsort)/sort | solution.py:19
  27.2 4.3 %compare_select_fusion.3 = s32[2048,1]{0,1:T(1,128)S(1)} fusion(s32[]{:T(128)} %bitcast.4, s32[]{:T(128)} %bitcast.5, s32[]{:T(128)} %bitcast.6, s32[]{:T(128)} %bitcast.7, s32[]{:T(128)} %bitcast.8, s32[]{:T(128)} %bitcast.10, s32[]{:T(128)} %bitcast.9, s32[2048,1]{0,1:T(1,128)S(1)} %get-tuple-element.12), kind=kLoop, calls=%fused_computation.34 | loop fusion | flops 30720 | bytes 16412 | tf_op jit(solution)/shard_map/gather | solution.py:22
  31.5 0.7 compare_and_fusion.1
  32.2 0.0 copy-start.2
  32.2 8.1 %scatter_custom_fusion.1 = s32[4096]{0:T(1024)S(1)} fusion(s32[2048]{0:T(1024)S(1)} %get-tuple-element.10, s32[2048]{0:T(1024)S(1)} %get-tuple-element.13, s32[]{:T(128)} %constant.26.clone.1), kind=kCustom, calls=%fused_computation.55 | custom fusion | bytes 16388 | tf_op jit(solution)/shard_map/scatter | solution.py:23
  40.3 8.9 %all_to_all.19 = s32[8,1,512]{2,1,0:T(1,128)S(1)} all-to-all(s32[8,1,512]{2,1,0:T(1,128)S(1)} %bitcast.43), channel_id=1, replica_groups=mesh['dp'=1,'ep'=8] {'ep'}, dimensions={0} | all-to-all | bytes 32768 | tf_op jit(solution)/shard_map/all_to_all | solution.py:24
  49.2 0.0 copy-start.1
  49.2 20.8 %gather_fusion = bf16[4096,768]{1,0:T(8,128)(2,1)} fusion(bf16[1024,768]{1,0:T(8,128)(2,1)} %param.5, s32[4096]{0:T(1024)S(1)} %broadcast_clamp_fusion), kind=kCustom, calls=%fused_computation | custom fusion | bytes 12599296 | tf_op jit(solution)/shard_map/jit(_take)/gather | solution.py:25
  70.0 0.0 copy-done.1
  70.0 6.7 %broadcast_select_fusion = bf16[8,512,768]{2,1,0:T(8,128)(2,1)} fusion(bf16[8,512,768]{2,1,0:T(8,128)(2,1)} %bitcast.37, pred[8,512]{1,0:T(8,128)(4,1)S(1)} %compare_and_fusion), kind=kLoop, calls=%fused_computation.23 | loop fusion | flops 3145728 | bytes 12587008 | tf_op jit(solution)/shard_map/jit(_take)/select_n | solution.py:25
  76.7 3.7 %all-to-all-start.1 = ((bf16[8,512,768]{2,1,0:T(8,128)(2,1)}), bf16[8,512,768]{2,1,0:T(8,128)(2,1)}, u32[]{:S(2)}, u32[]{:S(2)}) async-start(bf16[8,512,768]{2,1,0:T(8,128)(2,1)} %broadcast_select_fusion), calls=%async_computation.1 | async-start | bytes 12582912 | tf_op jit(solution)/shard_map/all_to_all | solution.py:26
  80.3 0.0 copy-done.2
  80.4 71.3 %all-to-all-done.1 = bf16[8,512,768]{2,1,0:T(8,128)(2,1)} async-done(((bf16[8,512,768]{2,1,0:T(8,128)(2,1)}), bf16[8,512,768]{2,1,0:T(8,128)(2,1)}, u32[]{:S(2)}, u32[]{:S(2)}) %all-to-all-start.1) | async-done | bytes 6291488 | tf_op jit(solution)/shard_map/all_to_all | solution.py:26
  151.6 0.0 copy-start.3
  151.6 12.1 %gather_fusion.1 = bf16[2048,768]{1,0:T(8,128)(2,1)S(1)} fusion(bf16[4096,768]{1,0:T(8,128)(2,1)} %bitcast.17, s32[2048]{0:T(1024)S(1)} %broadcast_clamp_fusion.1), kind=kCustom, calls=%fused_computation.1 | custom fusion | bytes 6299648 | tf_op jit(solution)/shard_map/jit(_take)/gather | solution.py:27
  163.7 0.0 copy-done.3
  163.7 30.7 %multiply_convert_fusion = bf16[8,256,768]{2,1,0:T(8,128)(2,1)} fusion(f32[8,256]{1,0:T(8,128)S(1)} %copy-done.3, bf16[8,3072,768]{2,1,0:T(8,128)(2,1)} %param.9, bf16[8,768,3072]{2,1,0:T(8,128)(2,1)} %param.8, bf16[8,256,768]{2,1,0:T(8,128)(2,1)S(1)} %bitcast.38, pred[8,256]{1,0:T(8,128)(4,1)S(1)} %broadcast_in_dim.44), kind=kOutput, calls=%fused_computation.22 | convolution fusion | flops 19388694528 | bytes 81799168 | tf_op jit(solution)/shard_map/ecf,efd->ecd/dot_general | solution.py:29
  194.4 14.0 %scatter_custom_fusion.2 = bf16[4096,768]{1,0:T(8,128)(2,1)} fusion(s32[2048]{0:T(1024)} %copy-done.2, bf16[2048,768]{1,0:T(8,128)(2,1)} %bitcast.50, bf16[]{:T(256)} %constant.63.clone.1), kind=kCustom, calls=%fused_computation.26 | custom fusion | bytes 6291968 | tf_op jit(solution)/shard_map/scatter | solution.py:31
  208.4 0.0 copy-start
  208.4 3.8 %all-to-all-start.2 = ((bf16[8,512,768]{2,1,0:T(8,128)(2,1)}), bf16[8,512,768]{2,1,0:T(8,128)(2,1)}, u32[]{:S(2)}, u32[]{:S(2)}) async-start(bf16[8,512,768]{2,1,0:T(8,128)(2,1)} %bitcast.36), calls=%async_computation.2 | async-start | bytes 12582912 | tf_op jit(solution)/shard_map/all_to_all | solution.py:32
  212.3 0.0 copy-done
  212.3 1.9 convert_element_type.18
  214.2 69.4 %all-to-all-done.2 = bf16[8,512,768]{2,1,0:T(8,128)(2,1)} async-done(((bf16[8,512,768]{2,1,0:T(8,128)(2,1)}), bf16[8,512,768]{2,1,0:T(8,128)(2,1)}, u32[]{:S(2)}, u32[]{:S(2)}) %all-to-all-start.2) | async-done | bytes 6291488 | tf_op jit(solution)/shard_map/all_to_all | solution.py:32
  283.5 31.8 %scatter_custom_fusion.3 = f32[1024,768]{1,0:T(8,128)} fusion(f32[1024,768]{1,0:T(8,128)} %convert_element_type.18, s32[4096]{0:T(1024)} %bitcast.40, bf16[4096,768]{1,0:T(8,128)(2,1)} %bitcast.22), kind=kCustom, calls=%fused_computation.16 | custom fusion | flops 6291456 | bytes 9437184 | tf_op jit(solution)/shard_map/scatter-add | solution.py:33
  315.3 3.2 convert_element_type.23
  (12 shorter events, 0.2 us)
Async XLA Ops:
  32.2 48.1 %copy-start.2 = (s32[2048]{0:T(1024)}, s32[2048]{0:T(1024)S(1)}, u32[]{:S(2)}) copy-start(s32[2048]{0:T(1024)S(1)} %get-tuple-element.10) | copy-start | bytes 24580
  49.2 20.8 %copy-start.1 = (s32[8,1,512]{2,1,0:T(1,128)}, s32[8,1,512]{2,1,0:T(1,128)S(1)}, u32[]{:S(2)}) copy-start(s32[8,1,512]{2,1,0:T(1,128)S(1)} %all_to_all.19) | copy-start | bytes 49156
  76.7 75.0 %all-to-all-start.1 = ((bf16[8,512,768]{2,1,0:T(8,128)(2,1)}), bf16[8,512,768]{2,1,0:T(8,128)(2,1)}, u32[]{:S(2)}, u32[]{:S(2)}) async-start(bf16[8,512,768]{2,1,0:T(8,128)(2,1)} %broadcast_select_fusion), calls=%async_computation.1 | async-start | bytes 12582912 | tf_op jit(solution)/shard_map/all_to_all | solution.py:26
  151.6 12.1 %copy-start.3 = (f32[8,256]{1,0:T(8,128)S(1)}, f32[8,256]{1,0:T(8,128)}, u32[]{:S(2)}) copy-start(f32[8,256]{1,0:T(8,128)} %param.7) | copy-start | bytes 24580
  208.4 3.8 %copy-start = (bf16[1024,768]{1,0:T(8,128)(2,1)S(1)}, bf16[1024,768]{1,0:T(8,128)(2,1)}, u32[]{:S(2)}) copy-start(bf16[1024,768]{1,0:T(8,128)(2,1)} %param.5) | copy-start | bytes 4718596
  208.4 75.1 %all-to-all-start.2 = ((bf16[8,512,768]{2,1,0:T(8,128)(2,1)}), bf16[8,512,768]{2,1,0:T(8,128)(2,1)}, u32[]{:S(2)}, u32[]{:S(2)}) async-start(bf16[8,512,768]{2,1,0:T(8,128)(2,1)} %bitcast.36), calls=%async_computation.2 | async-start | bytes 12582912 | tf_op jit(solution)/shard_map/all_to_all | solution.py:32
where the time goes:
time: 320 us; the launch traced here: 318 us
  waiting for transfers between devices  141 us (44%)
  other arithmetic  73.6 us (23%)
  local copies, waits for them, and re-layouts  57 us (18%)
  matrix products  30.7 us (10%)
  blocking collectives  8.86 us (3%)
  starting transfers between devices  7.5 us (2%)
    all_to_all x1, waiting for transfers between devices, local_layer(): lax.all_to_all(send_rows, 'ep', 0, 0, tiled=True)  71.3 us
    all_to_all x1, waiting for transfers between devices, local_layer(): lax.all_to_all(back_rows.reshape(group_size, pair_cap, model_width), 'ep'...  69.4 us
    scatter-add x1, other arithmetic, local_layer(): jax.ops.segment_sum(returned.astype(jnp.float32), wanted, num_segments=to...  31.8 us
    dot_general x1, matrix products, local_layer(): jnp.einsum('ecf,efd->ecd', hidden, down_loc, preferred_element_type=jnp.f...  30.7 us
    gather x1, local copies, waits for them, and re-layouts, local_layer(): jnp.take(x_loc, wanted, axis=0).reshape(group_size, pair_cap, model_width)  20.8 us
    scatter-add x1, other arithmetic, local_layer(): counts = jnp.bincount(src_dev, length=group_size)  14.7 us
    scatter x1, local copies, waits for them, and re-layouts, local_layer(): jnp.zeros((group_size * pair_cap, model_width), jnp.bfloat16).at[slot_idx]  14 us
    gather x1, local copies, waits for them, and re-layouts, local_layer(): jnp.take(received, slot_idx, axis=0).reshape(exp_loc, cap_rows, model_width)  12.1 us
  transfers between devices with their start and end apart: 2, of which 2 were waited for; matrix products, arithmetic and copies ran while one was open for 1% of the time, Pallas kernels for 0%

commit v1 on v0

v1 whole, which is shorter than its diff:
```python
import functools

import jax
import jax.numpy as jnp
from jax import lax
from jax.experimental import pallas as pl
from jax.experimental.pallas import tpu as pltpu
from jax.sharding import PartitionSpec as P

F32 = jnp.float32
BF16 = jnp.bfloat16
MESH = pl.DeviceIdType.MESH

NDEV = 8
CHUNKS = 8
LAG = 2


def _gelu(z):
    return 0.5 * z * (1.0 + jnp.tanh(0.7978845608028654 * (z + 0.044715 * (z * z * z))))


def _iota(shape, dim):
    return lax.broadcasted_iota(jnp.int32, shape, dim)


def _onehot(cond):
    return jnp.where(cond, 1.0, 0.0).astype(BF16)


def kernel(
    slots,
    x_ref, sel_ref, gate_ref, up_ref, down_ref,
    y_ref,
    xall, wup, wdn, send, ret, acc, pk, hid, pmat, yacc,
    sel_t, gate_t, code_s, rt_send, rt_recv, rowtab,
    own_sem, wup_sem, wdn_sem, agx_sem, agy_sem, ags_sem, agr_sem,
    rts_sem, rtr_sem, snd_sem, rcv_sem, loc_sem,
):
    n_exp, cap = sel_ref.shape
    tok, width = x_ref.shape
    ff = up_ref.shape[2]
    nslot = NDEV * slots
    me = lax.axis_index("ep")
    core = me % 2
    sib = me + 1 - 2 * core
    xx = (me // 2) % 2
    yy = me // 4
    dx = 2 - 4 * xx
    dy = 4 - 8 * yy
    xn, yn, dg = me + dx, me + dy, me + dx + dy
    peers = (dg, sib + dx + dy, xn, sib + dx, yn, sib + dy, sib)
    ch = tok // CHUNKS
    half = CHUNKS // 2

    def remote(src, dst, ssem, rsem, dev):
        return pltpu.make_async_remote_copy(
            src_ref=src, dst_ref=dst, send_sem=ssem, recv_sem=rsem, device_id={"ep": dev}, device_id_type=MESH
        )

    def up_copy(e):
        return pltpu.make_async_copy(up_ref.at[e], wup.at[e % 2], wup_sem.at[e % 2])

    def down_copy(e):
        return pltpu.make_async_copy(down_ref.at[e], wdn.at[e % 2], wdn_sem.at[e % 2])

    own_copy = pltpu.make_async_copy(x_ref, xall.at[me], own_sem)
    own_copy.start()

    barrier = pltpu.get_barrier_semaphore()
    for dev in peers:
        pl.semaphore_signal(barrier, inc=1, device_id={"ep": dev}, device_id_type=MESH)
    pl.semaphore_wait(barrier, NDEV - 1)
    own_copy.wait()

    def piece(owner, c):
        return xall.at[owner, pl.ds(c * ch, ch), :]

    def ag(owner, c, ssem, dev):
        return remote(piece(owner, c), piece(owner, c), ssem, agr_sem.at[owner, c], dev)

    sends = []

    def go(copy):
        copy.start()
        sends.append(copy)

    nx, ny, ns = 0, 0, 0
    for i in range(CHUNKS):
        go(ag(me, i, agx_sem.at[nx], xn))
        go(ag(me, (i + half) % CHUNKS, agy_sem.at[ny], yn))
        go(ag(me, i, ags_sem.at[ns], sib))
        nx, ny, ns = nx + 1, ny + 1, ns + 1

    for e in range(2):
        up_copy(e).start()
        down_copy(e).start()

    sel_t[...] = jnp.transpose(sel_ref[...].astype(F32))
    gate_t[...] = jnp.transpose(gate_ref[...])
    upper = _onehot(_iota((cap, cap), 0) < _iota((cap, cap), 1))
    for e in range(n_exp):
        sel_row = sel_ref[pl.ds(e, 1), :]
        owner = lax.shift_right_logical(sel_row, 10)
        local = jnp.bitwise_and(sel_row, 1023)
        mine = jnp.broadcast_to(owner, (16, cap)) == _iota((16, cap), 0)
        cum = jnp.dot(_onehot(mine), upper, preferred_element_type=F32)
        rank = jnp.sum(jnp.where(mine, cum, 0.0), axis=0, keepdims=True)
        owner_f = owner.astype(F32)
        code_s[pl.ds(e, 1), :] = owner_f * slots + rank
        tcode = (owner_f * 128 + rank).astype(jnp.int32) + core * slots
        q = _onehot(jnp.broadcast_to(tcode, (NDEV * 128, cap)) == _iota((NDEV * 128, cap), 0))
        hi = lax.shift_right_logical(local, 5).astype(F32)
        lo = jnp.bitwise_and(local, 31).astype(F32)
        rows = _iota((16, cap), 0)
        lhs = jnp.where(rows == 0, hi, jnp.where(rows == 1, lo, jnp.where(rows == 2, 1.0, 0.0))).astype(BF16)
        t = lax.dot_general(lhs, q, (((1,), (1,)), ((), ())), preferred_element_type=F32)
        tab = t[0:1] * 32.0 + t[1:2] + t[2:3]
        for g in range(NDEV):
            rt_send[g, pl.ds(e, 1), :] = tab[:, g * 128 : (g + 1) * 128]
    rt_recv[me] = rt_send[me]
    for k, dev in enumerate(peers):
        go(remote(rt_send.at[dev], rt_recv.at[me], rts_sem.at[k], rtr_sem.at[me], dev))

    for i in range(CHUNKS):
        cy = (i + half) % CHUNKS
        ag(xn, i, agx_sem.at[0], xn).wait_recv()
        ag(yn, cy, agy_sem.at[0], yn).wait_recv()
        if i < half:
            go(ag(xn, i, agy_sem.at[ny], yn))
            go(ag(yn, cy, agx_sem.at[nx], xn))
            nx, ny = nx + 1, ny + 1
        go(ag(xn, i, ags_sem.at[ns], sib))
        go(ag(yn, cy, ags_sem.at[ns + 1], sib))
        ns += 2
    for i in range(half):
        ag(dg, i, agy_sem.at[0], yn).wait_recv()
        ag(dg, i + half, agx_sem.at[0], xn).wait_recv()
        go(ag(dg, i, ags_sem.at[ns], sib))
        go(ag(dg, i + half, ags_sem.at[ns + 1], sib))
        ns += 2
    for dev in (sib, sib + dx, sib + dy, sib + dx + dy):
        for i in range(CHUNKS):
            ag(dev, i, ags_sem.at[0], sib).wait_recv()

    for k, dev in enumerate(peers):
        remote(rt_send.at[dev], rt_recv.at[dev], rts_sem.at[k], rtr_sem.at[dev], dev).wait_recv()
    for p in range(NDEV // 2):
        rowtab[:, p * 128 : (p + 1) * 128] = rt_recv[2 * p] + rt_recv[2 * p + 1] - 1.0
    yacc[...] = xall[me].astype(F32)

    def ret_copy(e, k, dev, src_dev):
        return remote(
            send.at[e, pl.ds(dev * slots, slots), :], ret.at[e, src_dev], snd_sem.at[e, k], rcv_sem.at[e, src_dev], dev
        )

    def loc_copy(e):
        return pltpu.make_async_copy(send.at[e, pl.ds(me * slots, slots), :], ret.at[e, me], loc_sem.at[e])

    def produce(e):
        lane8 = _iota((cap, n_exp), 1) == e
        selc = jnp.sum(jnp.where(lane8, sel_t[...], 0.0), axis=1, keepdims=True).astype(jnp.int32)
        gatec = jnp.sum(jnp.where(lane8, gate_t[...], 0.0), axis=1, keepdims=True)
        acc[...] = jnp.zeros_like(acc)

        def gather(b, carry):
            oh = _onehot(jnp.broadcast_to(selc - b * tok, (cap, tok)) == _iota((cap, tok), 1))
            acc[...] += jnp.dot(oh, xall[b], preferred_element_type=F32)
            return carry

        lax.fori_loop(0, NDEV, gather, 0)
        pk[...] = acc[...].astype(BF16)
        code = code_s[pl.ds(e, 1), :].astype(jnp.int32)
        pmat[...] = _onehot(jnp.broadcast_to(code, (nslot, cap)) == _iota((nslot, cap), 0))

        up_copy(e).wait()
        tile = 512

        def up(j, carry):
            cols = pl.ds(pl.multiple_of(j * tile, tile), tile)
            z = jnp.dot(pk[...], wup[e % 2, :, cols], preferred_element_type=F32)
            hid[:, cols] = _gelu(z).astype(BF16)
            return carry

        lax.fori_loop(0, ff // tile, up, 0)

        @pl.when(e + 2 < n_exp)
        def _():
            up_copy(e + 2).start()

        down_copy(e).wait()

        def down(j, carry):
            cols = pl.ds(pl.multiple_of(j * 256, 256), 256)
            o = jnp.dot(hid[...], wdn[e % 2, :, cols], preferred_element_type=F32)
            contrib = (o * gatec).astype(BF16)
            send[e, :, cols] = jnp.dot(pmat[...], contrib, preferred_element_type=F32).astype(BF16)
            return carry

        lax.fori_loop(0, width // 256, down, 0)

        @pl.when(e + 2 < n_exp)
        def _():
            down_copy(e + 2).start()

        for k, dev in enumerate(peers):
            ret_copy(e, k, dev, me).start()
        loc_copy(e).start()

    def combine(e):
        loc_copy(e).wait()
        for k, dev in enumerate(peers):
            ret_copy(e, k, dev, dev).wait_recv()
        row = rowtab[pl.ds(e, 1), :].astype(jnp.int32)
        tile = 256

        def add(j, carry):
            rows = pl.ds(pl.multiple_of(j * tile, tile), tile)
            s = _onehot(jnp.broadcast_to(row, (tile, nslot)) == _iota((tile, nslot), 0) + j * tile)
            yacc[rows, :] += jnp.dot(s, ret[e].reshape(nslot, width), preferred_element_type=F32)
            return carry

        lax.fori_loop(0, tok // tile, add, 0)

    def step(e, carry):
        produce(e)

        @pl.when(e >= LAG)
        def _():
            combine(e - LAG)

        return carry

    lax.fori_loop(0, n_exp, step, 0)

    def rest(e, carry):
        combine(e)
        return carry

    lax.fori_loop(n_exp - LAG, n_exp, rest, 0)
    y_ref[...] = yacc[...].astype(BF16)

    for copy in sends:
        copy.wait_send()

    def drain(e, carry):
        for k, dev in enumerate(peers):
            ret_copy(e, k, dev, me).wait_send()
        return carry

    lax.fori_loop(0, n_exp, drain, 0)


def solution(mesh):
    def local_layer(x_loc, sel_loc, gate_loc, up_loc, down_loc):
        tok, width = x_loc.shape
        n_exp, cap = sel_loc.shape
        ff = up_loc.shape[2]
        slots = 2 * cap // NDEV
        nslot = NDEV * slots
        dma = pltpu.SemaphoreType.DMA
        vmem = pl.BlockSpec(memory_space=pltpu.VMEM)
        hbm = pl.BlockSpec(memory_space=pl.ANY)
        return pl.pallas_call(
            functools.partial(kernel, slots),
            out_shape=jax.ShapeDtypeStruct((tok, width), BF16),
            in_specs=[hbm, vmem, vmem, hbm, hbm],
            out_specs=vmem,
            scratch_shapes=[
                pltpu.VMEM((NDEV, tok, width), BF16),
                pltpu.VMEM((2, width, ff), BF16),
                pltpu.VMEM((2, ff, width), BF16),
                pltpu.VMEM((n_exp, nslot, width), BF16),
                pltpu.VMEM((n_exp, NDEV, slots, width), BF16),
                pltpu.VMEM((cap, width), F32),
                pltpu.VMEM((cap, width), BF16),
                pltpu.VMEM((cap, ff), BF16),
                pltpu.VMEM((nslot, cap), BF16),
                pltpu.VMEM((tok, width), F32),
                pltpu.VMEM((cap, n_exp), F32),
                pltpu.VMEM((cap, n_exp), F32),
                pltpu.VMEM((n_exp, cap), F32),
                pltpu.VMEM((NDEV, n_exp, 128), F32),
                pltpu.VMEM((NDEV, n_exp, 128), F32),
                pltpu.VMEM((n_exp, nslot), F32),
                dma,
                dma((2,)),
                dma((2,)),
                dma((CHUNKS + CHUNKS // 2,)),
                dma((CHUNKS + CHUNKS // 2,)),
                dma((4 * CHUNKS,)),
                dma((NDEV, CHUNKS)),
                dma((NDEV - 1,)),
                dma((NDEV,)),
                dma((n_exp, NDEV - 1)),
                dma((n_exp, NDEV)),
                dma((n_exp,)),
            ],
            compiler_params=pltpu.CompilerParams(
                collective_id=0, has_side_effects=True, vmem_limit_bytes=67_000_000
            ),
            name="moe",
        )(x_loc, sel_loc, gate_loc, up_loc, down_loc)

    row_spec = P(("dp", "ep"), None)
    weight_spec = P("ep", None, None)
    return jax.shard_map(
        local_layer,
        mesh=mesh,
        in_specs=(row_spec, row_spec, row_spec, weight_spec, weight_spec),
        out_specs=row_spec,
        check_vma=False,
    )
```

time: 320 us -> 171 us (0.53)
  Pallas kernels: 0 us -> 168 us
  waiting for transfers between devices: 141 us -> 0 us
  other arithmetic: 73.6 us -> 0 us
  local copies, waits for them, and re-layouts: 57 us -> 2.65 us
  matrix products: 30.7 us -> 0 us
  blocking collectives: 8.86 us -> 0 us
  starting transfers between devices: 7.5 us -> 0 us
    pallas_call x0 -> x1, Pallas kernels: none -> 168 us  [local_layer(): pl.pallas_call(functools.partial(kernel, slots), out_shape=jax.ShapeDtype...]
    all_to_all x2 -> x0, waiting for transfers between devices: 141 us -> none  [the longest x1 71.3 us: local_layer(): lax.all_to_all(send_rows, 'ep', 0, 0, tiled=True)]
    scatter-add x2 -> x0, other arithmetic: 46.4 us -> none  [the longest x1 31.8 us: local_layer(): jax.ops.segment_sum(returned.astype(jnp.float32), wanted, num_segments=to...]
    gather x3 -> x0, local copies, waits for them, and re-layouts: 33.5 us -> none  [the longest x1 20.8 us: local_layer(): jnp.take(x_loc, wanted, axis=0).reshape(group_size, pair_cap, model_width)]
    dot_general x1 -> x0, matrix products: 30.7 us -> none  [local_layer(): jnp.einsum('ecf,efd->ecd', hidden, down_loc, preferred_element_type=jnp.f...]
    scatter x2 -> x0, local copies, waits for them, and re-layouts: 22.1 us -> none  [the longest x1 14 us: local_layer(): jnp.zeros((group_size * pair_cap, model_width), jnp.bfloat16).at[slot_idx]]
    sort x2 -> x0, other arithmetic: 10.1 us -> none  [the longest x1 5.04 us: local_layer(): position = jnp.argsort(sort_order)]
    all_to_all x1 -> x0, blocking collectives: 8.86 us -> none  [local_layer(): lax.all_to_all(request.reshape(group_size, pair_cap), 'ep', 0, 0, tiled=T...]
  transfers between devices with their start and end apart: 2 -> 0, of which waited for: 2 -> 0; matrix products, arithmetic and copies ran while one was open for 1% -> 0% of each run, Pallas kernels for 0% -> 0%
where the time goes in v1:
time: 171 us
  Pallas kernels  168 us (98%)
  local copies, waits for them, and re-layouts  2.65 us (2%)
    pallas_call x1, Pallas kernels, local_layer(): pl.pallas_call(functools.partial(kernel, slots), out_shape=jax.ShapeDtype...  168 us

profile of v1, /device:TPU:0, one launch (start us, length us, event | category | flops | bytes accessed | tf_op | source)
XLA Modules:
  0.0 170.8 jit_solution(1602485174794316136)
XLA Ops:
  0.0 168.2 %moe.1 = bf16[1024,768]{1,0:T(8,128)(2,1)} custom-call(bf16[1024,768]{1,0:T(8,128)(2,1)} %x_ref.1, s32[8,256]{1,0:T(8,128)} %sel_ref.1, f32[8,256]{1,0:T(8,128)} %gate_ref.1, bf16[8,768,3072]{2,1,0:T(8,128)(2,1)} %up_ref.1, bf16[8,3072,768]{2,1,0:T(8,128)(2,1)} %down_ref.1), custom_call_target="tpu_custom_call" | custom-call | tf_op jit(solution)/shard_map/moe/pallas_call | solution.py:264
  168.2 2.7 %copy.7 = bf16[1024,768]{1,0:T(8,128)(2,1)} copy(bf16[1024,768]{1,0:T(8,128)(2,1)} %moe.1) | data formatting | bytes 3145728

commit v2 on v1

--- a/solution.py
+++ b/solution.py
@@ -32,8 +32,8 @@
     slots,
     x_ref, sel_ref, gate_ref, up_ref, down_ref,
     y_ref,
-    xall, wup, wdn, send, ret, acc, pk, hid, pmat, yacc,
-    sel_t, gate_t, code_s, rt_send, rt_recv, rowtab,
+    xall, wup, wdn, send, ret, pk, hid, pmat, yacc,
+    sel_b, gate_b, code_s, rt_send, rt_recv, rowtab,
     own_sem, wup_sem, wdn_sem, agx_sem, agy_sem, ags_sem, agr_sem,
     rts_sem, rtr_sem, snd_sem, rcv_sem, loc_sem,
 ):
@@ -52,6 +52,7 @@
     peers = (dg, sib + dx + dy, xn, sib + dx, yn, sib + dy, sib)
     ch = tok // CHUNKS
     half = CHUNKS // 2
+    yorder = [*range(CHUNKS - 1, half - 1, -1), *range(half)]
 
     def remote(src, dst, ssem, rsem, dev):
         return pltpu.make_async_remote_copy(
@@ -88,7 +89,7 @@
     nx, ny, ns = 0, 0, 0
     for i in range(CHUNKS):
         go(ag(me, i, agx_sem.at[nx], xn))
-        go(ag(me, (i + half) % CHUNKS, agy_sem.at[ny], yn))
+        go(ag(me, yorder[i], agy_sem.at[ny], yn))
         go(ag(me, i, ags_sem.at[ns], sib))
         nx, ny, ns = nx + 1, ny + 1, ns + 1
 
@@ -96,8 +97,11 @@
         up_copy(e).start()
         down_copy(e).start()
 
-    sel_t[...] = jnp.transpose(sel_ref[...].astype(F32))
-    gate_t[...] = jnp.transpose(gate_ref[...])
+    sel_cols = jnp.transpose(sel_ref[...].astype(F32)).astype(jnp.int32)
+    gate_cols = jnp.transpose(gate_ref[...])
+    for e in range(n_exp):
+        sel_b[e * cap : (e + 1) * cap, :] = jnp.broadcast_to(sel_cols[:, e : e + 1], (cap, 128))
+        gate_b[e * cap : (e + 1) * cap, :] = jnp.broadcast_to(gate_cols[:, e : e + 1], (cap, 128))
     upper = _onehot(_iota((cap, cap), 0) < _iota((cap, cap), 1))
     for e in range(n_exp):
         sel_row = sel_ref[pl.ds(e, 1), :]
@@ -122,26 +126,85 @@
     for k, dev in enumerate(peers):
         go(remote(rt_send.at[dev], rt_recv.at[me], rts_sem.at[k], rtr_sem.at[me], dev))
 
-    for i in range(CHUNKS):
-        cy = (i + half) % CHUNKS
-        ag(xn, i, agx_sem.at[0], xn).wait_recv()
-        ag(yn, cy, agy_sem.at[0], yn).wait_recv()
+    def picks(rows, owner, first, depth):
+        n = rows.size
+        rel = sel_b[rows, :] - (owner * tok + first)
+        lane = _iota((n, 128), 1)
+        hot = jnp.concatenate([_onehot(rel == lane + g * 128) for g in range(depth // 128)], axis=1)
+        return jnp.dot(hot, xall[owner, first : first + depth, :], preferred_element_type=F32)
+
+    def gather(owner, first, depth, fresh=False):
+        n = 2 * cap
+
+        def some(i, carry):
+            rows = pl.ds(pl.multiple_of(i * n, n), n)
+            got = picks(rows, owner, first, depth).astype(BF16)
+            pk[rows, :] = got if fresh else pk[rows, :] + got
+            return carry
+
+        lax.fori_loop(0, n_exp * cap // n, some, 0)
+
+    def from_sib(owner, cs):
+        for c in cs:
+            ag(owner, c, ags_sem.at[0], sib).wait_recv()
+
+    xs, ys, ds = sib + dx, sib + dy, sib + dx + dy
+    hb = tok // 2
+    lo, hi = range(half), range(half, CHUNKS)
+
+    def slot(i):
+        nonlocal nx, ny, ns
+        if i < CHUNKS:
+            a, ca, b, cb = xn, i, yn, yorder[i]
+        else:
+            a, ca, b, cb = dg, i - CHUNKS, dg, yorder[i - CHUNKS]
+        ag(a, ca, agx_sem.at[0], xn).wait_recv()
+        ag(b, cb, agy_sem.at[0], yn).wait_recv()
         if i < half:
-            go(ag(xn, i, agy_sem.at[ny], yn))
-            go(ag(yn, cy, agx_sem.at[nx], xn))
+            go(ag(a, ca, agy_sem.at[ny], yn))
+            go(ag(b, cb, agx_sem.at[nx], xn))
             nx, ny = nx + 1, ny + 1
-        go(ag(xn, i, ags_sem.at[ns], sib))
-        go(ag(yn, cy, ags_sem.at[ns + 1], sib))
+        go(ag(a, ca, ags_sem.at[ns], sib))
+        go(ag(b, cb, ags_sem.at[ns + 1], sib))
         ns += 2
-    for i in range(half):
-        ag(dg, i, agy_sem.at[0], yn).wait_recv()
-        ag(dg, i + half, agx_sem.at[0], xn).wait_recv()
-        go(ag(dg, i, ags_sem.at[ns], sib))
-        go(ag(dg, i + half, ags_sem.at[ns + 1], sib))
-        ns += 2
-    for dev in (sib, sib + dx, sib + dy, sib + dx + dy):
-        for i in range(CHUNKS):
-            ag(dev, i, ags_sem.at[0], sib).wait_recv()
+
+    gather(me, 0, hb, True)
+    slot(0)
+    gather(me, hb, hb)
+    slot(1)
+    from_sib(sib, lo)
+    gather(sib, 0, hb)
+    slot(2)
+    from_sib(sib, hi)
+    gather(sib, hb, hb)
+    slot(3)
+    gather(xn, 0, hb)
+    slot(4)
+    gather(yn, hb, hb)
+    slot(5)
+    from_sib(xs, lo)
+    gather(xs, 0, hb)
+    slot(6)
+    from_sib(ys, hi)
+    gather(ys, hb, hb)
+    slot(7)
+    gather(xn, hb, hb)
+    slot(8)
+    gather(yn, 0, hb)
+    from_sib(xs, hi)
+    slot(9)
+    gather(xs, hb, hb)
+    slot(10)
+    from_sib(ys, lo)
+    gather(ys, 0, hb)
+    qb = hb // 2
+    gather(dg, 0, qb)
+    gather(dg, tok - qb, qb)
+    slot(11)
+    from_sib(ds, (0, 1, CHUNKS - 2, CHUNKS - 1))
+    gather(ds, 0, qb)
+    gather(ds, tok - qb, qb)
+    from_sib(ds, range(2, CHUNKS - 2))
 
     for k, dev in enumerate(peers):
         remote(rt_send.at[dev], rt_recv.at[dev], rts_sem.at[k], rtr_sem.at[dev], dev).wait_recv()
@@ -158,27 +221,18 @@
         return pltpu.make_async_copy(send.at[e, pl.ds(me * slots, slots), :], ret.at[e, me], loc_sem.at[e])
 
     def produce(e):
-        lane8 = _iota((cap, n_exp), 1) == e
-        selc = jnp.sum(jnp.where(lane8, sel_t[...], 0.0), axis=1, keepdims=True).astype(jnp.int32)
-        gatec = jnp.sum(jnp.where(lane8, gate_t[...], 0.0), axis=1, keepdims=True)
-        acc[...] = jnp.zeros_like(acc)
-
-        def gather(b, carry):
-            oh = _onehot(jnp.broadcast_to(selc - b * tok, (cap, tok)) == _iota((cap, tok), 1))
-            acc[...] += jnp.dot(oh, xall[b], preferred_element_type=F32)
-            return carry
-
-        lax.fori_loop(0, NDEV, gather, 0)
-        pk[...] = acc[...].astype(BF16)
+        rows = pl.ds(pl.multiple_of(e * cap, cap), cap)
+        late = picks(rows, dg, qb, hb) + picks(rows, ds, qb, hb)
+        pk[rows, :] = pk[rows, :] + late.astype(BF16)
         code = code_s[pl.ds(e, 1), :].astype(jnp.int32)
         pmat[...] = _onehot(jnp.broadcast_to(code, (nslot, cap)) == _iota((nslot, cap), 0))
 
         up_copy(e).wait()
-        tile = 512
+        tile = 1024
 
         def up(j, carry):
             cols = pl.ds(pl.multiple_of(j * tile, tile), tile)
-            z = jnp.dot(pk[...], wup[e % 2, :, cols], preferred_element_type=F32)
+            z = jnp.dot(pk[rows, :], wup[e % 2, :, cols], preferred_element_type=F32)
             hid[:, cols] = _gelu(z).astype(BF16)
             return carry
 
@@ -190,14 +244,10 @@
 
         down_copy(e).wait()
 
-        def down(j, carry):
-            cols = pl.ds(pl.multiple_of(j * 256, 256), 256)
-            o = jnp.dot(hid[...], wdn[e % 2, :, cols], preferred_element_type=F32)
-            contrib = (o * gatec).astype(BF16)
-            send[e, :, cols] = jnp.dot(pmat[...], contrib, preferred_element_type=F32).astype(BF16)
-            return carry
-
-        lax.fori_loop(0, width // 256, down, 0)
+        o = jnp.dot(hid[...], wdn[e % 2], preferred_element_type=F32)
+        gate = jnp.concatenate([gate_b[rows, :]] * (width // 128), axis=1)
+        contrib = (o * gate).astype(BF16)
+        send[e] = jnp.dot(pmat[...], contrib, preferred_element_type=F32).astype(BF16)
 
         @pl.when(e + 2 < n_exp)
         def _():
@@ -272,13 +322,12 @@
                 pltpu.VMEM((2, ff, width), BF16),
                 pltpu.VMEM((n_exp, nslot, width), BF16),
                 pltpu.VMEM((n_exp, NDEV, slots, width), BF16),
-                pltpu.VMEM((cap, width), F32),
-                pltpu.VMEM((cap, width), BF16),
+                pltpu.VMEM((n_exp * cap, width), BF16),
                 pltpu.VMEM((cap, ff), BF16),
                 pltpu.VMEM((nslot, cap), BF16),
                 pltpu.VMEM((tok, width), F32),
-                pltpu.VMEM((cap, n_exp), F32),
-                pltpu.VMEM((cap, n_exp), F32),
+                pltpu.VMEM((n_exp * cap, 128), jnp.int32),
+                pltpu.VMEM((n_exp * cap, 128), F32),
                 pltpu.VMEM((n_exp, cap), F32),
                 pltpu.VMEM((NDEV, n_exp, 128), F32),
                 pltpu.VMEM((NDEV, n_exp, 128), F32),

time: 171 us -> 144 us (0.84)
  Pallas kernels: 168 us -> 141 us
    pallas_call x1, Pallas kernels: 168 us -> 141 us  [local_layer(): pl.pallas_call(functools.partial(kernel, slots), out_shape=jax.ShapeDtype...]
where the time goes in v2:
time: 144 us
  Pallas kernels  141 us (98%)
  local copies, waits for them, and re-layouts  2.65 us (2%)
    pallas_call x1, Pallas kernels, local_layer(): pl.pallas_call(functools.partial(kernel, slots), out_shape=jax.ShapeDtype...  141 us

profile of v2, /device:TPU:0, one launch (start us, length us, event | category | flops | bytes accessed | tf_op | source)
XLA Modules:
  0.0 143.7 jit_solution(15959555665695556179)
XLA Ops:
  0.0 141.1 %moe.1 = bf16[1024,768]{1,0:T(8,128)(2,1)} custom-call(bf16[1024,768]{1,0:T(8,128)(2,1)} %x_ref.1, s32[8,256]{1,0:T(8,128)} %sel_ref.1, f32[8,256]{1,0:T(8,128)} %gate_ref.1, bf16[8,768,3072]{2,1,0:T(8,128)(2,1)} %up_ref.1, bf16[8,3072,768]{2,1,0:T(8,128)(2,1)} %down_ref.1), custom_call_target="tpu_custom_call" | custom-call | tf_op jit(solution)/shard_map/moe/pallas_call | solution.py:314
  141.1 2.7 %copy.7 = bf16[1024,768]{1,0:T(8,128)(2,1)} copy(bf16[1024,768]{1,0:T(8,128)(2,1)} %moe.1) | data formatting | bytes 3145728

commit v3 on v2

--- a/solution.py
+++ b/solution.py
@@ -13,7 +13,6 @@
 
 NDEV = 8
 CHUNKS = 8
-LAG = 2
 
 
 def _gelu(z):
@@ -32,10 +31,10 @@
     slots,
     x_ref, sel_ref, gate_ref, up_ref, down_ref,
     y_ref,
-    xall, wup, wdn, send, ret, pk, hid, pmat, yacc,
+    xall, wup, wdn, send, ret, pk, hid, dpk, yacc,
     sel_b, gate_b, code_s, rt_send, rt_recv, rowtab,
     own_sem, wup_sem, wdn_sem, agx_sem, agy_sem, ags_sem, agr_sem,
-    rts_sem, rtr_sem, snd_sem, rcv_sem, loc_sem,
+    rts_sem, rtr_sem, snd_sem, rcv_sem, loc_sem, out_sem,
 ):
     n_exp, cap = sel_ref.shape
     tok, width = x_ref.shape
@@ -69,9 +68,9 @@
     own_copy.start()
 
     barrier = pltpu.get_barrier_semaphore()
-    for dev in peers:
+    for dev in (sib, xn, yn):
         pl.semaphore_signal(barrier, inc=1, device_id={"ep": dev}, device_id_type=MESH)
-    pl.semaphore_wait(barrier, NDEV - 1)
+    pl.semaphore_wait(barrier, 3)
     own_copy.wait()
 
     def piece(owner, c):
@@ -123,9 +122,7 @@
         for g in range(NDEV):
             rt_send[g, pl.ds(e, 1), :] = tab[:, g * 128 : (g + 1) * 128]
     rt_recv[me] = rt_send[me]
-    for k, dev in enumerate(peers):
-        go(remote(rt_send.at[dev], rt_recv.at[me], rts_sem.at[k], rtr_sem.at[me], dev))
-
+    yacc[...] = xall[me].astype(F32)
     def picks(rows, owner, first, depth):
         n = rows.size
         rel = sel_b[rows, :] - (owner * tok + first)
@@ -133,7 +130,7 @@
         hot = jnp.concatenate([_onehot(rel == lane + g * 128) for g in range(depth // 128)], axis=1)
         return jnp.dot(hot, xall[owner, first : first + depth, :], preferred_element_type=F32)
 
-    def gather(owner, first, depth, fresh=False):
+    def gather(owner, first, depth, pairs=(0, n_exp // 2), fresh=False):
         n = 2 * cap
 
         def some(i, carry):
@@ -142,7 +139,7 @@
             pk[rows, :] = got if fresh else pk[rows, :] + got
             return carry
 
-        lax.fori_loop(0, n_exp * cap // n, some, 0)
+        lax.fori_loop(*pairs, some, 0)
 
     def from_sib(owner, cs):
         for c in cs:
@@ -168,7 +165,111 @@
         go(ag(b, cb, ags_sem.at[ns + 1], sib))
         ns += 2
 
-    gather(me, 0, hb, True)
+    def ret_copy(e, k, src_dev):
+        dev = peers[k]
+        return remote(
+            send.at[e, pl.ds(dev * slots, slots), :], ret.at[e, src_dev], snd_sem.at[e, k], rcv_sem.at[e, src_dev], dev
+        )
+
+    def loc_copy(e):
+        return pltpu.make_async_copy(send.at[e, pl.ds(me * slots, slots), :], ret.at[e, me], loc_sem.at[e])
+
+    def up(lhs, m, e):
+        up_copy(e).wait()
+        tile = 1024
+
+        def some(j, carry):
+            cols = pl.ds(pl.multiple_of(j * tile, tile), tile)
+            z = jnp.dot(lhs[...], wup[e % 2, :, cols], preferred_element_type=F32)
+            hid[0:m, cols] = _gelu(z).astype(BF16)
+            return carry
+
+        lax.fori_loop(0, ff // tile, some, 0)
+
+    def scatter(e, rows):
+        code = code_s[pl.ds(e, 1), :].astype(jnp.int32)
+        place = _onehot(jnp.broadcast_to(code, (nslot, cap)) == _iota((nslot, cap), 0))
+        o = jnp.dot(hid[...], wdn[e % 2], preferred_element_type=F32)
+        gate = jnp.concatenate([gate_b[rows, :]] * (width // 128), axis=1)
+        contrib = (o * gate).astype(BF16)
+        send[e] = jnp.dot(place, contrib, preferred_element_type=F32).astype(BF16)
+
+    def early(e):
+        rows = pl.ds(e * cap, cap)
+        up(pk.at[rows, :], cap, e)
+        down_copy(e).wait()
+        scatter(e, rows)
+        for k in range(2, NDEV - 1):
+            ret_copy(e, k, me).start()
+        loc_copy(e).start()
+
+    def diagonal(e, carry):
+        rows = pl.ds(pl.multiple_of(e * cap, cap), cap)
+        m = 2 * slots
+        base = pl.multiple_of((dg // 2) * m, m)
+        code = code_s[pl.ds(e, 1), :].astype(jnp.int32) - base
+        here = jnp.broadcast_to(code, (m, cap)) == _iota((m, cap), 0)
+        gate = jnp.sum(jnp.where(here, gate_ref[pl.ds(e, 1), :], 0.0), axis=1, keepdims=True)
+        dpk[...] = jnp.dot(_onehot(here), pk[rows, :], preferred_element_type=F32).astype(BF16)
+        tile = 1024
+
+        def some(j, c):
+            cols = pl.ds(pl.multiple_of(j * tile, tile), tile)
+            z = jnp.dot(dpk[...], wup[e % 2, :, cols], preferred_element_type=F32)
+            hid[0:m, cols] = _gelu(z).astype(BF16)
+            return c
+
+        lax.fori_loop(0, ff // tile, some, 0)
+        up_copy(e + 2).start()
+        o = jnp.dot(hid[0:m, :], wdn[e % 2], preferred_element_type=F32)
+        send[e, pl.ds(base, m), :] = (o * gate).astype(BF16)
+        down_copy(e + 2).start()
+        for k in range(2):
+            ret_copy(e, k, me).start()
+        return carry
+
+    def produce(e):
+        rows = pl.ds(pl.multiple_of(e * cap, cap), cap)
+        up(pk.at[rows, :], cap, e)
+
+        @pl.when(e + 2 < n_exp)
+        def _():
+            up_copy(e + 2).start()
+
+        down_copy(e).wait()
+        scatter(e, rows)
+
+        @pl.when(e + 2 < n_exp)
+        def _():
+            down_copy(e + 2).start()
+
+        for k in range(NDEV - 1):
+            ret_copy(e, k, me).start()
+        loc_copy(e).start()
+
+    def arrived(e):
+        loc_copy(e).wait()
+        for k, dev in enumerate(peers):
+            ret_copy(e, k, dev).wait_recv()
+
+    def adds(e, j, tile):
+        row = rowtab[pl.ds(e, 1), :].astype(jnp.int32)
+        hot = _onehot(jnp.broadcast_to(row, (tile, nslot)) == _iota((tile, nslot), 0) + j * tile)
+        return jnp.dot(hot, ret[e].reshape(nslot, width), preferred_element_type=F32)
+
+    def combine(e):
+        arrived(e)
+        tile = 256
+
+        def some(j, carry):
+            rows = pl.ds(pl.multiple_of(j * tile, tile), tile)
+            yacc[rows, :] += adds(e, j, tile)
+            return carry
+
+        lax.fori_loop(0, tok // tile, some, 0)
+
+    qb = hb // 2
+    gather(me, 0, hb, fresh=True)
     slot(0)
     gather(me, hb, hb)
     slot(1)
@@ -179,126 +280,97 @@
     gather(sib, hb, hb)
     slot(3)
     gather(xn, 0, hb)
+    from_sib(xs, lo)
     slot(4)
+    for k, dev in enumerate(peers):
+        go(remote(rt_send.at[dev], rt_recv.at[me], rts_sem.at[k], rtr_sem.at[me], dev))
     gather(yn, hb, hb)
+    gather(xs, 0, hb)
     slot(5)
-    from_sib(xs, lo)
-    gather(xs, 0, hb)
-    slot(6)
     from_sib(ys, hi)
     gather(ys, hb, hb)
+    gather(xn, hb, qb)
+    slot(6)
+    gather(yn, 0, qb)
+    from_sib(xs, (4, 5))
+    gather(xs, hb, qb)
+    from_sib(ys, (0, 1))
+    gather(ys, 0, qb)
     slot(7)
-    gather(xn, hb, hb)
+    first, later = (0, 1), (1, n_exp // 2)
+
+    def third(pairs):
+        gather(xn, hb + qb, qb, pairs)
+        gather(yn, qb, qb, pairs)
+        gather(xs, hb + qb, qb, pairs)
+        gather(ys, qb, qb, pairs)
+
+    from_sib(xs, (6, 7))
+    from_sib(ys, (2, 3))
+    third(first)
+    early(0)
     slot(8)
-    gather(yn, 0, hb)
-    from_sib(xs, hi)
+    early(1)
     slot(9)
-    gather(xs, hb, hb)
+    third(later)
     slot(10)
-    from_sib(ys, lo)
-    gather(ys, 0, hb)
-    qb = hb // 2
-    gather(dg, 0, qb)
-    gather(dg, tok - qb, qb)
+    from_sib(ds, (0, 1, CHUNKS - 2, CHUNKS - 1))
+    for dev in (dg, ds):
+        gather(dev, 0, qb, first)
+        gather(dev, tok - qb, qb, first)
     slot(11)
-    from_sib(ds, (0, 1, CHUNKS - 2, CHUNKS - 1))
-    gather(ds, 0, qb)
-    gather(ds, tok - qb, qb)
     from_sib(ds, range(2, CHUNKS - 2))
+    for dev in (dg, ds):
+        gather(dev, qb, hb, first)
+
+    lax.fori_loop(0, 2, diagonal, 0)
 
     for k, dev in enumerate(peers):
         remote(rt_send.at[dev], rt_recv.at[dev], rts_sem.at[k], rtr_sem.at[dev], dev).wait_recv()
     for p in range(NDEV // 2):
         rowtab[:, p * 128 : (p + 1) * 128] = rt_recv[2 * p] + rt_recv[2 * p + 1] - 1.0
-    yacc[...] = xall[me].astype(F32)
-
-    def ret_copy(e, k, dev, src_dev):
-        return remote(
-            send.at[e, pl.ds(dev * slots, slots), :], ret.at[e, src_dev], snd_sem.at[e, k], rcv_sem.at[e, src_dev], dev
-        )
-
-    def loc_copy(e):
-        return pltpu.make_async_copy(send.at[e, pl.ds(me * slots, slots), :], ret.at[e, me], loc_sem.at[e])
-
-    def produce(e):
-        rows = pl.ds(pl.multiple_of(e * cap, cap), cap)
-        late = picks(rows, dg, qb, hb) + picks(rows, ds, qb, hb)
-        pk[rows, :] = pk[rows, :] + late.astype(BF16)
-        code = code_s[pl.ds(e, 1), :].astype(jnp.int32)
-        pmat[...] = _onehot(jnp.broadcast_to(code, (nslot, cap)) == _iota((nslot, cap), 0))
-
-        up_copy(e).wait()
-        tile = 1024
-
-        def up(j, carry):
-            cols = pl.ds(pl.multiple_of(j * tile, tile), tile)
-            z = jnp.dot(pk[rows, :], wup[e % 2, :, cols], preferred_element_type=F32)
-            hid[:, cols] = _gelu(z).astype(BF16)
-            return carry
-
-        lax.fori_loop(0, ff // tile, up, 0)
-
-        @pl.when(e + 2 < n_exp)
+
+    def pair(p, carry):
+        for dev in (dg, ds):
+            gather(dev, 0, tok, (p, p + 1))
+        produce(2 * p)
+
+        @pl.when(p >= 2)
         def _():
-            up_copy(e + 2).start()
-
-        down_copy(e).wait()
-
-        o = jnp.dot(hid[...], wdn[e % 2], preferred_element_type=F32)
-        gate = jnp.concatenate([gate_b[rows, :]] * (width // 128), axis=1)
-        contrib = (o * gate).astype(BF16)
-        send[e] = jnp.dot(pmat[...], contrib, preferred_element_type=F32).astype(BF16)
-
-        @pl.when(e + 2 < n_exp)
-        def _():
-            down_copy(e + 2).start()
-
-        for k, dev in enumerate(peers):
-            ret_copy(e, k, dev, me).start()
-        loc_copy(e).start()
-
-    def combine(e):
-        loc_copy(e).wait()
-        for k, dev in enumerate(peers):
-            ret_copy(e, k, dev, dev).wait_recv()
-        row = rowtab[pl.ds(e, 1), :].astype(jnp.int32)
-        tile = 256
-
-        def add(j, carry):
-            rows = pl.ds(pl.multiple_of(j * tile, tile), tile)
-            s = _onehot(jnp.broadcast_to(row, (tile, nslot)) == _iota((tile, nslot), 0) + j * tile)
-            yacc[rows, :] += jnp.dot(s, ret[e].reshape(nslot, width), preferred_element_type=F32)
-            return carry
-
-        lax.fori_loop(0, tok // tile, add, 0)
-
-    def step(e, carry):
-        produce(e)
-
-        @pl.when(e >= LAG)
-        def _():
-            combine(e - LAG)
-
+            combine(2 * p - 3)
+
+        produce(2 * p + 1)
+        combine(2 * p - 2)
         return carry
 
-    lax.fori_loop(0, n_exp, step, 0)
+    lax.fori_loop(1, n_exp // 2, pair, 0)
 
     def rest(e, carry):
         combine(e)
         return carry
 
-    lax.fori_loop(n_exp - LAG, n_exp, rest, 0)
-    y_ref[...] = yacc[...].astype(BF16)
+    lax.fori_loop(n_exp - 3, n_exp - 1, rest, 0)
+    last = n_exp - 1
+    arrived(last)
+    tile = 256
+    outs = []
+    for j in range(tok // tile):
+        rows = pl.ds(j * tile, tile)
+        pk[rows, :] = (yacc[rows, :] + adds(last, j, tile)).astype(BF16)
+        outs.append(pltpu.make_async_copy(pk.at[rows, :], y_ref.at[rows, :], out_sem.at[j]))
+        outs[-1].start()
 
     for copy in sends:
         copy.wait_send()
 
     def drain(e, carry):
-        for k, dev in enumerate(peers):
-            ret_copy(e, k, dev, me).wait_send()
+        for k in range(NDEV - 1):
+            ret_copy(e, k, me).wait_send()
         return carry
 
     lax.fori_loop(0, n_exp, drain, 0)
+    for copy in outs:
+        copy.wait()
 
 
 def solution(mesh):
@@ -315,7 +387,7 @@
             functools.partial(kernel, slots),
             out_shape=jax.ShapeDtypeStruct((tok, width), BF16),
             in_specs=[hbm, vmem, vmem, hbm, hbm],
-            out_specs=vmem,
+            out_specs=hbm,
             scratch_shapes=[
                 pltpu.VMEM((NDEV, tok, width), BF16),
                 pltpu.VMEM((2, width, ff), BF16),
@@ -324,7 +396,7 @@
                 pltpu.VMEM((n_exp, NDEV, slots, width), BF16),
                 pltpu.VMEM((n_exp * cap, width), BF16),
                 pltpu.VMEM((cap, ff), BF16),
-                pltpu.VMEM((nslot, cap), BF16),
+                pltpu.VMEM((2 * slots, width), BF16),
                 pltpu.VMEM((tok, width), F32),
                 pltpu.VMEM((n_exp * cap, 128), jnp.int32),
                 pltpu.VMEM((n_exp * cap, 128), F32),
@@ -344,6 +416,7 @@
                 dma((n_exp, NDEV - 1)),
                 dma((n_exp, NDEV)),
                 dma((n_exp,)),
+                dma((4,)),
             ],
             compiler_params=pltpu.CompilerParams(
                 collective_id=0, has_side_effects=True, vmem_limit_bytes=67_000_000

time: 144 us -> 132 us (0.917)
  Pallas kernels: 141 us -> 130 us
    pallas_call x1, Pallas kernels: 141 us -> 130 us  [local_layer(): pl.pallas_call(functools.partial(kernel, slots), out_shape=jax.ShapeDtype...]
where the time goes in v3:
time: 132 us
  Pallas kernels  130 us (98%)
  local copies, waits for them, and re-layouts  2.65 us (2%)
    pallas_call x1, Pallas kernels, local_layer(): pl.pallas_call(functools.partial(kernel, slots), out_shape=jax.ShapeDtype...  130 us
    unnamed x1, local copies, waits for them, and re-layouts  2.65 us

profile of v3, /device:TPU:0, one launch (start us, length us, event | category | flops | bytes accessed | tf_op | source)
XLA Modules:
  0.0 132.3 jit_solution(10676587977328540557)
XLA Ops:
  0.0 129.6 %moe.1 = bf16[1024,768]{1,0:T(8,128)(2,1)} custom-call(bf16[1024,768]{1,0:T(8,128)(2,1)} %x_ref.1, s32[8,256]{1,0:T(8,128)} %sel_ref.1, f32[8,256]{1,0:T(8,128)} %gate_ref.1, bf16[8,768,3072]{2,1,0:T(8,128)(2,1)} %up_ref.1, bf16[8,3072,768]{2,1,0:T(8,128)(2,1)} %down_ref.1), custom_call_target="tpu_custom_call" | custom-call | tf_op jit(solution)/shard_map/moe/pallas_call | solution.py:386
  129.6 2.7 %copy.7 = bf16[1024,768]{1,0:T(8,128)(2,1)} copy(bf16[1024,768]{1,0:T(8,128)(2,1)} %moe.1) | data formatting | bytes 3145728

commit v4 on v3

--- a/solution.py
+++ b/solution.py
@@ -29,12 +29,12 @@
 
 def kernel(
     slots,
-    x_ref, sel_ref, gate_ref, up_ref, down_ref,
+    x_ref, sel_hbm, gate_hbm, up_ref, down_ref,
     y_ref,
-    xall, wup, wdn, send, ret, pk, hid, dpk, yacc,
+    sel_ref, gate_ref, xall, wup, wdn, send, ret, pk, hid, dpk, yacc,
     sel_b, gate_b, code_s, rt_send, rt_recv, rowtab,
     own_sem, wup_sem, wdn_sem, agx_sem, agy_sem, ags_sem, agr_sem,
-    rts_sem, rtr_sem, snd_sem, rcv_sem, loc_sem, out_sem,
+    rts_sem, rtr_sem, snd_sem, rcv_sem, loc_sem, in_sem,
 ):
     n_exp, cap = sel_ref.shape
     tok, width = x_ref.shape
@@ -66,6 +66,10 @@
 
     own_copy = pltpu.make_async_copy(x_ref, xall.at[me], own_sem)
     own_copy.start()
+    sel_copy = pltpu.make_async_copy(sel_hbm, sel_ref, in_sem.at[0])
+    gate_copy = pltpu.make_async_copy(gate_hbm, gate_ref, in_sem.at[1])
+    sel_copy.start()
+    gate_copy.start()
 
     barrier = pltpu.get_barrier_semaphore()
     for dev in (sib, xn, yn):
@@ -95,6 +99,9 @@
     for e in range(2):
         up_copy(e).start()
         down_copy(e).start()
+
+    sel_copy.wait()
+    gate_copy.wait()
 
     sel_cols = jnp.transpose(sel_ref[...].astype(F32)).astype(jnp.int32)
     gate_cols = jnp.transpose(gate_ref[...])
@@ -353,12 +360,13 @@
     last = n_exp - 1
     arrived(last)
     tile = 256
-    outs = []
-    for j in range(tok // tile):
-        rows = pl.ds(j * tile, tile)
-        pk[rows, :] = (yacc[rows, :] + adds(last, j, tile)).astype(BF16)
-        outs.append(pltpu.make_async_copy(pk.at[rows, :], y_ref.at[rows, :], out_sem.at[j]))
-        outs[-1].start()
+
+    def finish(j, carry):
+        rows = pl.ds(pl.multiple_of(j * tile, tile), tile)
+        y_ref[rows, :] = (yacc[rows, :] + adds(last, j, tile)).astype(BF16)
+        return carry
+
+    lax.fori_loop(0, tok // tile, finish, 0)
 
     for copy in sends:
         copy.wait_send()
@@ -369,8 +377,6 @@
         return carry
 
     lax.fori_loop(0, n_exp, drain, 0)
-    for copy in outs:
-        copy.wait()
 
 
 def solution(mesh):
@@ -385,10 +391,12 @@
         hbm = pl.BlockSpec(memory_space=pl.ANY)
         return pl.pallas_call(
             functools.partial(kernel, slots),
-            out_shape=jax.ShapeDtypeStruct((tok, width), BF16),
-            in_specs=[hbm, vmem, vmem, hbm, hbm],
-            out_specs=hbm,
+            out_shape=pltpu.VMEM((tok, width), BF16),
+            in_specs=[hbm] * 5,
+            out_specs=vmem,
             scratch_shapes=[
+                pltpu.VMEM((n_exp, cap), jnp.int32),
+                pltpu.VMEM((n_exp, cap), F32),
                 pltpu.VMEM((NDEV, tok, width), BF16),
                 pltpu.VMEM((2, width, ff), BF16),
                 pltpu.VMEM((2, ff, width), BF16),
@@ -416,10 +424,10 @@
                 dma((n_exp, NDEV - 1)),
                 dma((n_exp, NDEV)),
                 dma((n_exp,)),
-                dma((4,)),
+                dma((2,)),
             ],
             compiler_params=pltpu.CompilerParams(
-                collective_id=0, has_side_effects=True, vmem_limit_bytes=67_000_000
+                collective_id=0, has_side_effects=True, vmem_limit_bytes=64_000_000
             ),
             name="moe",
         )(x_loc, sel_loc, gate_loc, up_loc, down_loc)

time: 132 us -> 130 us (0.985)
  local copies, waits for them, and re-layouts: 2.65 us -> 1.15 us
    unnamed x1, local copies, waits for them, and re-layouts: 2.65 us -> 1.15 us
where the time goes in v4:
time: 130 us
  Pallas kernels  129 us (99%)
    pallas_call x1, Pallas kernels, local_layer(): pl.pallas_call(functools.partial(kernel, slots), out_shape=pltpu.VMEM((to...  129 us

profile of v4, /device:TPU:0, one launch (start us, length us, event | category | flops | bytes accessed | tf_op | source)
XLA Modules:
  0.0 130.0 jit_solution(10133950631949044001)
XLA Ops:
  0.0 128.9 %moe.1 = bf16[1024,768]{1,0:T(8,128)(2,1)S(1)} custom-call(bf16[1024,768]{1,0:T(8,128)(2,1)} %x_ref.1, s32[8,256]{1,0:T(8,128)} %sel_hbm.1, f32[8,256]{1,0:T(8,128)} %gate_hbm.1, bf16[8,768,3072]{2,1,0:T(8,128)(2,1)} %up_ref.1, bf16[8,3072,768]{2,1,0:T(8,128)(2,1)} %down_ref.1), custom_call_target="tpu_custom_call" | custom-call | tf_op jit(solution)/shard_map/moe/pallas_call | solution.py:392
  128.9 1.1 copy.7

commit v5 on v4

--- a/solution.py
+++ b/solution.py
@@ -33,8 +33,7 @@
     y_ref,
     sel_ref, gate_ref, xall, wup, wdn, send, ret, pk, hid, dpk, yacc,
     sel_b, gate_b, code_s, rt_send, rt_recv, rowtab,
-    own_sem, wup_sem, wdn_sem, agx_sem, agy_sem, ags_sem, agr_sem,
-    rts_sem, rtr_sem, snd_sem, rcv_sem, loc_sem, in_sem,
+    in_sem, wup_sem, wdn_sem, ag_snd, ag_sem, sib_sem, rt_snd, rt_sem, snd_sem, rcv_sem,
 ):
     n_exp, cap = sel_ref.shape
     tok, width = x_ref.shape
@@ -64,7 +63,7 @@
     def down_copy(e):
         return pltpu.make_async_copy(down_ref.at[e], wdn.at[e % 2], wdn_sem.at[e % 2])
 
-    own_copy = pltpu.make_async_copy(x_ref, xall.at[me], own_sem)
+    own_copy = pltpu.make_async_copy(x_ref, xall.at[me], in_sem.at[2])
     own_copy.start()
     sel_copy = pltpu.make_async_copy(sel_hbm, sel_ref, in_sem.at[0])
     gate_copy = pltpu.make_async_copy(gate_hbm, gate_ref, in_sem.at[1])
@@ -80,21 +79,16 @@
     def piece(owner, c):
         return xall.at[owner, pl.ds(c * ch, ch), :]
 
-    def ag(owner, c, ssem, dev):
-        return remote(piece(owner, c), piece(owner, c), ssem, agr_sem.at[owner, c], dev)
-
-    sends = []
-
-    def go(copy):
-        copy.start()
-        sends.append(copy)
-
-    nx, ny, ns = 0, 0, 0
+    def take(ref, sem):
+        pltpu.make_async_copy(ref, ref, sem).wait()
+
+    def ag(owner, c, sem, dev):
+        remote(piece(owner, c), piece(owner, c), ag_snd, sem, dev).start()
+
     for i in range(CHUNKS):
-        go(ag(me, i, agx_sem.at[nx], xn))
-        go(ag(me, yorder[i], agy_sem.at[ny], yn))
-        go(ag(me, i, ags_sem.at[ns], sib))
-        nx, ny, ns = nx + 1, ny + 1, ns + 1
+        ag(me, i, ag_sem.at[i], xn)
+        ag(me, yorder[i], ag_sem.at[i], yn)
+        ag(me, i, sib_sem.at[i // half], sib)
 
     for e in range(2):
         up_copy(e).start()
@@ -148,38 +142,32 @@
 
         lax.fori_loop(*pairs, some, 0)
 
-    def from_sib(owner, cs):
-        for c in cs:
-            ag(owner, c, ags_sem.at[0], sib).wait_recv()
+    def from_sib(group):
+        take(xall.at[sib, pl.ds(0, half * ch), :], sib_sem.at[group])
 
     xs, ys, ds = sib + dx, sib + dy, sib + dx + dy
     hb = tok // 2
-    lo, hi = range(half), range(half, CHUNKS)
 
     def slot(i):
-        nonlocal nx, ny, ns
+        take(xall.at[xn, pl.ds(0, 2 * ch), :], ag_sem.at[i])
         if i < CHUNKS:
             a, ca, b, cb = xn, i, yn, yorder[i]
         else:
             a, ca, b, cb = dg, i - CHUNKS, dg, yorder[i - CHUNKS]
-        ag(a, ca, agx_sem.at[0], xn).wait_recv()
-        ag(b, cb, agy_sem.at[0], yn).wait_recv()
         if i < half:
-            go(ag(a, ca, agy_sem.at[ny], yn))
-            go(ag(b, cb, agx_sem.at[nx], xn))
-            nx, ny = nx + 1, ny + 1
-        go(ag(a, ca, ags_sem.at[ns], sib))
-        go(ag(b, cb, ags_sem.at[ns + 1], sib))
-        ns += 2
-
-    def ret_copy(e, k, src_dev):
+            ag(a, ca, ag_sem.at[CHUNKS + i], yn)
+            ag(b, cb, ag_sem.at[CHUNKS + i], xn)
+        ga = (2, 2, 2, 2, 4, 4, 5, 5, 6, 6, 7, 7)[i]
+        gb = (3, 3, 3, 3, 4, 4, 5, 5, 6, 6, 7, 7)[i]
+        ag(a, ca, sib_sem.at[ga], sib)
+        ag(b, cb, sib_sem.at[gb], sib)
+
+    def ret_copy(e, k):
         dev = peers[k]
-        return remote(
-            send.at[e, pl.ds(dev * slots, slots), :], ret.at[e, src_dev], snd_sem.at[e, k], rcv_sem.at[e, src_dev], dev
-        )
+        return remote(send.at[e, pl.ds(dev * slots, slots), :], ret.at[e, me], snd_sem, rcv_sem.at[e], dev)
 
     def loc_copy(e):
-        return pltpu.make_async_copy(send.at[e, pl.ds(me * slots, slots), :], ret.at[e, me], loc_sem.at[e])
+        return pltpu.make_async_copy(send.at[e, pl.ds(me * slots, slots), :], ret.at[e, me], rcv_sem.at[e])
 
     def up(lhs, m, e):
         up_copy(e).wait()
@@ -207,7 +195,7 @@
         down_copy(e).wait()
         scatter(e, rows)
         for k in range(2, NDEV - 1):
-            ret_copy(e, k, me).start()
+            ret_copy(e, k).start()
         loc_copy(e).start()
 
     def diagonal(e, carry):
@@ -232,7 +220,7 @@
         send[e, pl.ds(base, m), :] = (o * gate).astype(BF16)
         down_copy(e + 2).start()
         for k in range(2):
-            ret_copy(e, k, me).start()
+            ret_copy(e, k).start()
         return carry
 
     def produce(e):
@@ -251,13 +239,11 @@
             down_copy(e + 2).start()
 
         for k in range(NDEV - 1):
-            ret_copy(e, k, me).start()
+            ret_copy(e, k).start()
         loc_copy(e).start()
 
     def arrived(e):
-        loc_copy(e).wait()
-        for k, dev in enumerate(peers):
-            ret_copy(e, k, dev).wait_recv()
+        take(ret.at[e], rcv_sem.at[e])
 
     def adds(e, j, tile):
         row = rowtab[pl.ds(e, 1), :].astype(jnp.int32)
@@ -280,28 +266,27 @@
     slot(0)
     gather(me, hb, hb)
     slot(1)
-    from_sib(sib, lo)
+    from_sib(0)
     gather(sib, 0, hb)
     slot(2)
-    from_sib(sib, hi)
+    from_sib(1)
     gather(sib, hb, hb)
     slot(3)
     gather(xn, 0, hb)
-    from_sib(xs, lo)
+    from_sib(2)
     slot(4)
-    for k, dev in enumerate(peers):
-        go(remote(rt_send.at[dev], rt_recv.at[me], rts_sem.at[k], rtr_sem.at[me], dev))
+    for dev in peers:
+        remote(rt_send.at[dev], rt_recv.at[me], rt_snd, rt_sem, dev).start()
     gather(yn, hb, hb)
     gather(xs, 0, hb)
     slot(5)
-    from_sib(ys, hi)
+    from_sib(3)
     gather(ys, hb, hb)
     gather(xn, hb, qb)
     slot(6)
     gather(yn, 0, qb)
-    from_sib(xs, (4, 5))
+    from_sib(4)
     gather(xs, hb, qb)
-    from_sib(ys, (0, 1))
     gather(ys, 0, qb)
     slot(7)
     first, later = (0, 1), (1, n_exp // 2)
@@ -312,8 +297,7 @@
         gather(xs, hb + qb, qb, pairs)
         gather(ys, qb, qb, pairs)
 
-    from_sib(xs, (6, 7))
-    from_sib(ys, (2, 3))
+    from_sib(5)
     third(first)
     early(0)
     slot(8)
@@ -321,19 +305,18 @@
     slot(9)
     third(later)
     slot(10)
-    from_sib(ds, (0, 1, CHUNKS - 2, CHUNKS - 1))
+    from_sib(6)
     for dev in (dg, ds):
         gather(dev, 0, qb, first)
         gather(dev, tok - qb, qb, first)
     slot(11)
-    from_sib(ds, range(2, CHUNKS - 2))
+    from_sib(7)
     for dev in (dg, ds):
         gather(dev, qb, hb, first)
 
     lax.fori_loop(0, 2, diagonal, 0)
 
-    for k, dev in enumerate(peers):
-        remote(rt_send.at[dev], rt_recv.at[dev], rts_sem.at[k], rtr_sem.at[dev], dev).wait_recv()
+    take(rt_recv.at[pl.ds(0, NDEV - 1)], rt_sem)
     for p in range(NDEV // 2):
         rowtab[:, p * 128 : (p + 1) * 128] = rt_recv[2 * p] + rt_recv[2 * p + 1] - 1.0
 
@@ -368,15 +351,9 @@
 
     lax.fori_loop(0, tok // tile, finish, 0)
 
-    for copy in sends:
-        copy.wait_send()
-
-    def drain(e, carry):
-        for k in range(NDEV - 1):
-            ret_copy(e, k, me).wait_send()
-        return carry
-
-    lax.fori_loop(0, n_exp, drain, 0)
+    take(xall.at[pl.ds(0, 7)], ag_snd)
+    take(rt_send.at[pl.ds(0, NDEV - 1)], rt_snd)
+    take(send.at[pl.ds(0, n_exp * (NDEV - 1) // NDEV)], snd_sem)
 
 
 def solution(mesh):
@@ -412,19 +389,16 @@
                 pltpu.VMEM((NDEV, n_exp, 128), F32),
                 pltpu.VMEM((NDEV, n_exp, 128), F32),
                 pltpu.VMEM((n_exp, nslot), F32),
-                dma,
+                dma((3,)),
                 dma((2,)),
                 dma((2,)),
+                dma,
                 dma((CHUNKS + CHUNKS // 2,)),
-                dma((CHUNKS + CHUNKS // 2,)),
-                dma((4 * CHUNKS,)),
-                dma((NDEV, CHUNKS)),
-                dma((NDEV - 1,)),
-                dma((NDEV,)),
-                dma((n_exp, NDEV - 1)),
-                dma((n_exp, NDEV)),
+                dma((8,)),
+                dma,
+                dma,
+                dma,
                 dma((n_exp,)),
-                dma((2,)),
             ],
             compiler_params=pltpu.CompilerParams(
                 collective_id=0, has_side_effects=True, vmem_limit_bytes=64_000_000

time: 130 us -> 128 us (0.985)
  Pallas kernels: 129 us -> 127 us
    pallas_call x1, Pallas kernels: 129 us -> 127 us  [local_layer(): pl.pallas_call(functools.partial(kernel, slots), out_shape=pltpu.VMEM((to...]
where the time goes in v5:
time: 128 us
  Pallas kernels  127 us (99%)
    pallas_call x1, Pallas kernels, local_layer(): pl.pallas_call(functools.partial(kernel, slots), out_shape=pltpu.VMEM((to...  127 us

profile of v5, /device:TPU:0, one launch (start us, length us, event | category | flops | bytes accessed | tf_op | source)
XLA Modules:
  0.0 127.7 jit_solution(13477702856080665225)
XLA Ops:
  0.0 126.6 %moe.1 = bf16[1024,768]{1,0:T(8,128)(2,1)S(1)} custom-call(bf16[1024,768]{1,0:T(8,128)(2,1)} %x_ref.1, s32[8,256]{1,0:T(8,128)} %sel_hbm.1, f32[8,256]{1,0:T(8,128)} %gate_hbm.1, bf16[8,768,3072]{2,1,0:T(8,128)(2,1)} %up_ref.1, bf16[8,3072,768]{2,1,0:T(8,128)(2,1)} %down_ref.1), custom_call_target="tpu_custom_call" | custom-call | tf_op jit(solution)/shard_map/moe/pallas_call | solution.py:369
  126.6 1.1 copy.7

commit v6 on v5

--- a/solution.py
+++ b/solution.py
@@ -166,6 +166,11 @@
         dev = peers[k]
         return remote(send.at[e, pl.ds(dev * slots, slots), :], ret.at[e, me], snd_sem, rcv_sem.at[e], dev)
 
+    last, hs = n_exp - 1, slots // 2
+
+    def half_refs(dev, h):
+        return send.at[last, pl.ds(dev * slots + h * hs, hs), :], ret.at[last, me, pl.ds(h * hs, hs), :]
+
     def loc_copy(e):
         return pltpu.make_async_copy(send.at[e, pl.ds(me * slots, slots), :], ret.at[e, me], rcv_sem.at[e])
 
@@ -238,9 +243,20 @@
         def _():
             down_copy(e + 2).start()
 
-        for k in range(NDEV - 1):
-            ret_copy(e, k).start()
-        loc_copy(e).start()
+        @pl.when(e < last)
+        def _():
+            for k in range(NDEV - 1):
+                ret_copy(e, k).start()
+            loc_copy(e).start()
+
+        @pl.when(e == last)
+        def _():
+            for h in range(2):
+                for dev in peers:
+                    src, dst = half_refs(dev, h)
+                    remote(src, dst, snd_sem, rcv_sem.at[last + h], dev).start()
+                src, dst = half_refs(me, h)
+                pltpu.make_async_copy(src, dst, rcv_sem.at[last + h]).start()
 
     def arrived(e):
         take(ret.at[e], rcv_sem.at[e])
@@ -340,16 +356,21 @@
         return carry
 
     lax.fori_loop(n_exp - 3, n_exp - 1, rest, 0)
-    last = n_exp - 1
-    arrived(last)
-    tile = 256
-
-    def finish(j, carry):
-        rows = pl.ds(pl.multiple_of(j * tile, tile), tile)
-        y_ref[rows, :] = (yacc[rows, :] + adds(last, j, tile)).astype(BF16)
-        return carry
-
-    lax.fori_loop(0, tok // tile, finish, 0)
+    row = rowtab[pl.ds(last, 1), :].astype(jnp.int32)
+    for h in range(2):
+        picks_h = [row[:, d * slots + h * hs : d * slots + (h + 1) * hs] for d in range(NDEV)]
+        lanes = jnp.concatenate(picks_h, axis=1)
+        take(ret.at[last, pl.ds(0, NDEV // 2)], rcv_sem.at[last + h])
+        tile = 512
+        for j in range(tok // tile):
+            rows = pl.ds(j * tile, tile)
+            hot = _onehot(jnp.broadcast_to(lanes, (tile, nslot // 2)) == _iota((tile, nslot // 2), 0) + j * tile)
+            back = ret[last, :, h * hs : (h + 1) * hs, :].reshape(nslot // 2, width)
+            total = yacc[rows, :] + jnp.dot(hot, back, preferred_element_type=F32)
+            if h == 0:
+                yacc[rows, :] = total
+            else:
+                y_ref[rows, :] = total.astype(BF16)
 
     take(xall.at[pl.ds(0, 7)], ag_snd)
     take(rt_send.at[pl.ds(0, NDEV - 1)], rt_snd)
@@ -398,7 +419,7 @@
                 dma,
                 dma,
                 dma,
-                dma((n_exp,)),
+                dma((n_exp + 1,)),
             ],
             compiler_params=pltpu.CompilerParams(
                 collective_id=0, has_side_effects=True, vmem_limit_bytes=64_000_000

time: 128 us -> 127 us (level)
  no operation moved by 1% of the time
where the time goes in v6:
time: 127 us
  Pallas kernels  126 us (99%)
    pallas_call x1, Pallas kernels, local_layer(): pl.pallas_call(functools.partial(kernel, slots), out_shape=pltpu.VMEM((to...  126 us

profile of v6, /device:TPU:0, one launch (start us, length us, event | category | flops | bytes accessed | tf_op | source)
XLA Modules:
  0.0 126.8 jit_solution(17151557586249555831)
XLA Ops:
  0.0 125.6 %moe.1 = bf16[1024,768]{1,0:T(8,128)(2,1)S(1)} custom-call(bf16[1024,768]{1,0:T(8,128)(2,1)} %x_ref.1, s32[8,256]{1,0:T(8,128)} %sel_hbm.1, f32[8,256]{1,0:T(8,128)} %gate_hbm.1, bf16[8,768,3072]{2,1,0:T(8,128)(2,1)} %up_ref.1, bf16[8,3072,768]{2,1,0:T(8,128)(2,1)} %down_ref.1), custom_call_target="tpu_custom_call" | custom-call | tf_op jit(solution)/shard_map/moe/pallas_call | solution.py:390
  125.7 1.1 copy.7

commit v7 on v6

--- a/solution.py
+++ b/solution.py
@@ -167,6 +167,7 @@
         return remote(send.at[e, pl.ds(dev * slots, slots), :], ret.at[e, me], snd_sem, rcv_sem.at[e], dev)
 
     last, hs = n_exp - 1, slots // 2
+    spread = (2, 0, 4, 3, 1, 5, 6)
 
     def half_refs(dev, h):
         return send.at[last, pl.ds(dev * slots + h * hs, hs), :], ret.at[last, me, pl.ds(h * hs, hs), :]
@@ -245,14 +246,14 @@
 
         @pl.when(e < last)
         def _():
-            for k in range(NDEV - 1):
+            for k in spread:
                 ret_copy(e, k).start()
             loc_copy(e).start()
 
         @pl.when(e == last)
         def _():
             for h in range(2):
-                for dev in peers:
+                for dev in [peers[k] for k in spread]:
                     src, dst = half_refs(dev, h)
                     remote(src, dst, snd_sem, rcv_sem.at[last + h], dev).start()
                 src, dst = half_refs(me, h)

time: 127 us -> 126 us (level)
  no operation moved by 1% of the time
where the time goes in v7:
time: 126 us
  Pallas kernels  125 us (99%)
    pallas_call x1, Pallas kernels, local_layer(): pl.pallas_call(functools.partial(kernel, slots), out_shape=pltpu.VMEM((to...  125 us

profile of v7, /device:TPU:0, one launch (start us, length us, event | category | flops | bytes accessed | tf_op | source)
XLA Modules:
  0.0 126.1 jit_solution(13374982398609668770)
XLA Ops:
  0.0 125.0 %moe.1 = bf16[1024,768]{1,0:T(8,128)(2,1)S(1)} custom-call(bf16[1024,768]{1,0:T(8,128)(2,1)} %x_ref.1, s32[8,256]{1,0:T(8,128)} %sel_hbm.1, f32[8,256]{1,0:T(8,128)} %gate_hbm.1, bf16[8,768,3072]{2,1,0:T(8,128)(2,1)} %up_ref.1, bf16[8,3072,768]{2,1,0:T(8,128)(2,1)} %down_ref.1), custom_call_target="tpu_custom_call" | custom-call | tf_op jit(solution)/shard_map/moe/pallas_call | solution.py:391
  125.0 1.1 copy.7

commit v8 on v7

--- a/solution.py
+++ b/solution.py
@@ -252,10 +252,11 @@
 
         @pl.when(e == last)
         def _():
+            turns = ((2, 0), (0, 0), (4, 0), (0, 1), (3, 0), (1, 0), (5, 0), (1, 1), (2, 1), (4, 1), (3, 1), (5, 1), (6, 0), (6, 1))
+            for k, h in turns:
+                src, dst = half_refs(peers[k], h)
+                remote(src, dst, snd_sem, rcv_sem.at[last + h], peers[k]).start()
             for h in range(2):
-                for dev in [peers[k] for k in spread]:
-                    src, dst = half_refs(dev, h)
-                    remote(src, dst, snd_sem, rcv_sem.at[last + h], dev).start()
                 src, dst = half_refs(me, h)
                 pltpu.make_async_copy(src, dst, rcv_sem.at[last + h]).start()
 

time: 126 us -> 127 us (level)
  no operation moved by 1% of the time
where the time goes in v8:
time: 127 us
  Pallas kernels  126 us (99%)
    pallas_call x1, Pallas kernels, local_layer(): pl.pallas_call(functools.partial(kernel, slots), out_shape=pltpu.VMEM((to...  126 us

profile of v8, /device:TPU:0, one launch (start us, length us, event | category | flops | bytes accessed | tf_op | source)
XLA Modules:
  0.0 126.7 jit_solution(2047860594336908297)
XLA Ops:
  0.0 125.5 %moe.1 = bf16[1024,768]{1,0:T(8,128)(2,1)S(1)} custom-call(bf16[1024,768]{1,0:T(8,128)(2,1)} %x_ref.1, s32[8,256]{1,0:T(8,128)} %sel_hbm.1, f32[8,256]{1,0:T(8,128)} %gate_hbm.1, bf16[8,768,3072]{2,1,0:T(8,128)(2,1)} %up_ref.1, bf16[8,3072,768]{2,1,0:T(8,128)(2,1)} %down_ref.1), custom_call_target="tpu_custom_call" | custom-call | tf_op jit(solution)/shard_map/moe/pallas_call | solution.py:392
  125.5 1.1 copy.7
